TPU v7x, 32 devices: a whole 2x2x4 slice. The times are simulated.
32 devices in a mesh: gx: 4 (over z), gy: 4 (over x, core), col: 2 (over y).
Axes of the slice: x: 2, y: 2, z: 4, core: 2. Of those that a mesh axis runs over, the one named last changes fastest.
Arguments:
- fields: bfloat16 [2, 128, 128, 32, 128], P('col', 'gx', 'gy'), may hold values from -6 to 6
- spectral: bfloat16 [1, 16, 16, 2, 32, 32, 16], P(None, 'gx', 'gy', None, None, 'col'), may hold values from -0.75 to 0.75
- skip_weight: bfloat16 [1, 32, 32], replicated, may hold values from -1 to 1
- skip_bias: float32 [1, 32], replicated, may hold values from -3 to 3
- norm_gain: float32 [1, 32], replicated, may hold values from 0.5 to 1.5
- norm_shift: float32 [1, 32], replicated, may hold values from -3 to 3
Outputs:
- activations: bfloat16 [2, 128, 128, 32, 128], P('col', 'gx', 'gy')
All inputs are finite; a program needn't handle non-finite values.
Results may differ from a plain program's by a relative error of at most 0.012.
Values may be sent and summed in bfloat16 or wider, within the bound.
A program may use at most 128 MiB of HBM per device.

v0:
```python
import math
import jax
import jax.numpy as jnp
from jax import lax
from jax.sharding import PartitionSpec as P

X = 128
Y = 128
Z = 128
MX = 16
MY = 16
MZ = 16
norm_eps = 1e-05


def signed_freqs(count):
    index = jnp.arange(count, dtype=jnp.int32)
    return jnp.where(index < count // 2, index, index - count)


def angles(positions, frequency, length):
    turn_count = positions[:, None] * frequency[None, :] % length
    return turn_count.astype(jnp.float32) * (2.0 * math.pi / length)


def forward_table(positions, frequency, length, factor):
    phase_angle = angles(positions, frequency, length)
    cosine = jnp.cos(phase_angle) * factor
    sine_part = jnp.sin(phase_angle) * factor
    from_real = jnp.stack([cosine, -sine_part], axis=-1)
    from_imag = jnp.stack([sine_part, cosine], axis=-1)
    return jnp.stack([from_real, from_imag], axis=1)


def inverse_table(frequency, positions, length):
    phase_angle = angles(positions, frequency, length).T
    cosine = jnp.cos(phase_angle)
    sine_part = jnp.sin(phase_angle)
    from_real = jnp.stack([cosine, sine_part], axis=-1)
    from_imag = jnp.stack([-sine_part, cosine], axis=-1)
    return jnp.stack([from_real, from_imag], axis=1)


def depth_tables(length, count):
    frequency = jnp.arange(count, dtype=jnp.int32)
    phase_angle = angles(jnp.arange(length, dtype=jnp.int32), frequency, length)
    forward = jnp.concatenate([jnp.cos(phase_angle), -jnp.sin(phase_angle)], axis=1)
    backward = jnp.concatenate([jnp.cos(phase_angle).T, -jnp.sin(phase_angle).T], axis=0)
    return (forward.astype(jnp.bfloat16), backward.astype(jnp.bfloat16))


def mix_modes(spectrum, weight):

    def contract(left, right):
        return jnp.einsum("abcz,abcdz->abdz", left, right, preferred_element_type=jnp.float32)

    real_in = spectrum[:, :, :, 0]
    imag_in = spectrum[:, :, :, 1]
    real_weight = weight[:, :, 0]
    imag_weight = weight[:, :, 1]
    real_out = contract(real_in, real_weight) - contract(imag_in, imag_weight)
    imag_out = contract(real_in, imag_weight) + contract(imag_in, real_weight)
    return jnp.stack([real_out, imag_out], axis=3)


def finish(spectral_part, skip_part, offset, scaling, shift_term):
    pre_norm = spectral_part + skip_part + offset[:, None]
    centre = jnp.mean(pre_norm, axis=2, keepdims=True)
    spread = jnp.mean(jnp.square(pre_norm - centre), axis=2, keepdims=True)
    normed = (pre_norm - centre) * lax.rsqrt(spread + norm_eps) * scaling[:, None] + shift_term[
        :, None
    ]
    return jax.nn.gelu(normed, approximate=False).astype(jnp.bfloat16)


def local(fields, spectral, skip_weight, skip_bias, norm_gain, norm_shift):
    highest = lax.Precision.HIGHEST
    hidden = fields[0]
    tile_first, tile_second, channels, depth_cells = hidden.shape
    first_cells = lax.axis_index("gx") * tile_first + jnp.arange(tile_first, dtype=jnp.int32)
    second_cells = lax.axis_index("gy") * tile_second + jnp.arange(tile_second, dtype=jnp.int32)
    depth_forward, depth_backward = depth_tables(Z, MZ)
    second_forward = forward_table(second_cells, signed_freqs(MY), Y, 1.0).astype(jnp.bfloat16)
    first_forward = forward_table(first_cells, signed_freqs(MX), X, 1.0 / math.sqrt(X * Y * Z))
    first_inverse = inverse_table(signed_freqs(MX), first_cells, X).astype(jnp.bfloat16)
    second_inverse = inverse_table(signed_freqs(MY), second_cells, Y)
    inverse_scale = 1.0 / math.sqrt(MX * MY * MZ)
    amplitude = jnp.dot(
        hidden.reshape(-1, depth_cells), depth_forward, preferred_element_type=jnp.float32
    )
    amplitude = amplitude.astype(jnp.bfloat16).reshape(tile_first, tile_second, channels, 2, MZ)
    along_second = jnp.einsum(
        "xycrz,yrks->xkcsz", amplitude, second_forward, preferred_element_type=jnp.float32
    )
    summed_second = lax.psum_scatter(
        along_second.astype(jnp.bfloat16), "gy", scatter_dimension=1, tiled=True
    ).astype(jnp.float32)
    partial_modes = jnp.einsum("xkcsz,xsjt->jkctz", summed_second, first_forward, precision=highest)
    summed = lax.psum_scatter(
        partial_modes.astype(jnp.bfloat16), "gx", scatter_dimension=0, tiled=True
    )
    weights_here = spectral[0]
    mixed_modes = mix_modes(summed, lax.all_gather(weights_here, "col", axis=4, tiled=True)).astype(
        jnp.bfloat16
    )
    gathered_second = lax.all_gather(mixed_modes, "gy", axis=1, tiled=True)
    full_modes = lax.all_gather(gathered_second, "gx", axis=0, tiled=True)
    rows_first = jnp.einsum(
        "jkcsz,jsxt->xkctz", full_modes, first_inverse, preferred_element_type=jnp.float32
    )
    rows_both = jnp.einsum(
        "xkcsz,ksyt->xyctz", rows_first, second_inverse, precision=highest
    ).astype(jnp.bfloat16)
    spectral_part = jnp.dot(
        rows_both.reshape(-1, 2 * MZ), depth_backward, preferred_element_type=jnp.float32
    )
    spectral_part = (
        spectral_part.reshape(tile_first, tile_second, channels, depth_cells) * inverse_scale
    )
    skip_part = jnp.einsum(
        "oc,xycz->xyoz", skip_weight[0], hidden, preferred_element_type=jnp.float32
    )
    hidden = finish(spectral_part, skip_part, skip_bias[0], norm_gain[0], norm_shift[0])
    return hidden[None]


def solution(mesh):
    placed = (
        P("col", "gx", "gy", None, None),
        P(None, "gx", "gy", None, None, "col", None),
        P(),
        P(),
        P(),
        P(),
    )
    return jax.shard_map(
        local,
        mesh=mesh,
        in_specs=placed,
        out_specs=P("col", "gx", "gy", None, None),
        check_vma=False,
    )
```

profile of v0, /device:TPU:0, one launch (start us, length us, event | category | flops | bytes accessed | tf_op | source)
XLA Modules:
  0.0 268.1 jit_solution(5952482807343169716)
XLA Ops:
  7.4 0.1 negate_convert_fusion.1
  7.4 6.4 %fusion = bf16[32768,32]{0,1:T(8,128)(2,1)S(1)} fusion(bf16[32768,128]{1,0:T(8,128)(2,1)} %bitcast.159, bf16[128,16]{0,1:T(8,128)(2,1)S(1)} %get-tuple-element.37, bf16[128,16]{0,1:T(8,128)(2,1)S(1)} %get-tuple-element.38), kind=kOutput, calls=%fused_computation.1 | convolution fusion | flops 269500416 | bytes 10493952 | tf_op jit(solution)/shard_map/dot_general | solution.py:88
  13.8 7.9 %reshape.722 = bf16[32,32,32,2,16]{2,1,0,4,3:T(8,128)(2,1)} reshape(bf16[32768,32]{0,1:T(8,128)(2,1)S(1)} %fusion) | data formatting | bytes 4194304 | tf_op jit(solution)/shard_map/reshape | solution.py:91
  21.7 0.2 fusion.88
  21.9 4.7 %fusion.24 = bf16[32,16,32,2,16]{2,1,4,0,3:T(8,128)(2,1)S(1)} fusion(bf16[32,32,32,2,16]{2,1,0,4,3:T(8,128)(2,1)} %reshape.722, bf16[32,1,16,2]{0,2,1,3:T(8,128)(2,1)S(1)} %get-tuple-element.16, bf16[32,1,16,2]{0,2,1,3:T(8,128)(2,1)S(1)} %get-tuple-element.15), kind=kOutput, calls=%fused_computation.37 | convolution fusion | flops 67641344 | bytes 3149824 | tf_op jit(solution)/shard_map/xycrz,yrks->xkcsz/dot_general | solution.py:92
  26.6 3.1 %copy.26 = bf16[32,16,32,2,16]{2,4,3,0,1:T(8,128)(2,1)} copy(bf16[32,16,32,2,16]{2,1,4,0,3:T(8,128)(2,1)S(1)} %fusion.24) | data formatting | bytes 2097152 | tf_op jit(solution)/shard_map/convert_element_type | solution.py:96
  29.8 0.5 all-gather.3.cloned.1.call-update
  30.3 0.2 reduce-scatter.5.cloned.1.call-start
  30.5 0.1 negate_convert_fusion
  30.6 0.2 fusion.85
  30.8 15.1 %fusion.13 = f32[32,32,128,32]{2,3,1,0:T(8,128)} fusion(bf16[1,32,32,32,128]{4,3,2,1,0:T(8,128)(2,1)} %param.6, bf16[1,32,32]{2,1,0:T(8,128)(2,1)S(1)} %copy-done), kind=kOutput, calls=%fused_computation.27 | convolution fusion | flops 268435456 | bytes 25167872 | tf_op jit(solution)/shard_map/oc,xycz->xyoz/dot_general | solution.py:120
  46.0 31.2 %reduce-scatter.3.cloned.1.call-done = bf16[32,4,32,2,16]{2,4,3,0,1:T(8,128)(2,1)} async-done(((bf16[32,16,32,2,16]{2,4,3,0,1:T(8,128)(2,1)}), bf16[32,4,32,2,16]{2,4,3,0,1:T(8,128)(2,1)}) %reduce-scatter.3.cloned.1.call-update) | async-done | bytes 262160 | tf_op jit(solution)/shard_map/reduce_scatter | solution.py:95
  77.2 1.9 fusion.30
  79.1 0.9 copy.29
  80.1 11.0 %all-gather.3.cloned.1.call-done = bf16[1,4,4,2,32,32,16]{4,6,5,3,2,1,0:T(8,128)(2,1)} async-done(((bf16[1,4,4,2,32,16,16]{4,6,5,3,2,1,0:T(8,128)(2,1)}), bf16[1,4,4,2,32,32,16]{4,6,5,3,2,1,0:T(8,128)(2,1)}) %all-gather.3.cloned.1.call-update) | async-done | bytes 1048592 | tf_op jit(solution)/shard_map/all_gather | solution.py:103
  91.1 4.5 %slice_bitcast_fusion = (bf16[4,4,32,32,16]{2,4,3,1,0:T(8,128)(2,1)}, bf16[4,4,32,32,16]{2,4,3,1,0:T(8,128)(2,1)S(1)}) fusion(bf16[4,4,2,32,32,16]{3,5,4,2,1,0:T(8,128)(2,1)} %bitcast.161), kind=kLoop, calls=%fused_computation.39 | loop fusion | bytes 2097152 | tf_op jit(solution)/shard_map/squeeze | solution.py:60
  95.6 4.5 %copy.44 = bf16[4,4,32,32,16]{3,2,4,1,0:T(8,128)(2,1)} copy(bf16[4,4,32,32,16]{2,4,3,1,0:T(8,128)(2,1)} %get-tuple-element.5) | data formatting | bytes 1048576 | tf_op jit(solution)/shard_map/squeeze | solution.py:60
  100.2 2.9 %copy.41 = bf16[4,4,32,32,16]{3,2,4,1,0:T(8,128)(2,1)} copy(bf16[4,4,32,32,16]{2,4,3,1,0:T(8,128)(2,1)S(1)} %get-tuple-element.6) | data formatting | bytes 1048576 | tf_op jit(solution)/shard_map/squeeze | solution.py:59
  103.1 0.9 slice_bitcast_fusion.3
  104.0 2.2 fusion.39
  106.2 2.3 fusion.37
  108.5 2.3 fusion.35
  110.7 2.2 fusion.41
  113.1 7.2 %all_gather.10 = bf16[4,16,32,2,16]{2,4,3,0,1:T(8,128)(2,1)S(1)} all-gather(bf16[4,4,32,2,16]{2,4,3,0,1:T(8,128)(2,1)S(1)} %pad_maximum_fusion), channel_id=1, replica_groups=mesh['gx'=4,'gy'=4,'col'=2] {'gy'}, dimensions={1}, use_global_device_ids=true | all-gather | bytes 163840 | tf_op jit(solution)/shard_map/all_gather | solution.py:106
  120.3 38.6 %all_gather.11 = bf16[16,16,32,2,16]{2,4,3,1,0:T(8,128)(2,1)S(1)} all-gather(bf16[4,16,32,2,16]{2,4,3,1,0:T(8,128)(2,1)S(1)} %copy.30), channel_id=1, replica_groups=mesh['gx'=4,'gy'=4,'col'=2] {'gx'}, dimensions={0}, use_global_device_ids=true | all-gather | bytes 655360 | tf_op jit(solution)/shard_map/all_gather | solution.py:107
  158.8 1.5 convolution_bitcast_fusion
  160.3 22.8 %fusion.12 = bf16[32,32,32,2,16]{2,1,4,0,3:T(8,128)(2,1)} fusion(f32[32,16,32,2,16]{2,0,4,1,3:T(8,128)S(1)} %convolution_bitcast_fusion, f32[16,1,32,2]{2,0,3,1:T(8,128)S(1)} %get-tuple-element.10, f32[16,1,32,2]{2,0,3,1:T(8,128)S(1)} %get-tuple-element.9), kind=kOutput, calls=%fused_computation.26 | convolution fusion | flops 403703808 | bytes 4202496 | tf_op jit(solution)/shard_map/xkcsz,ksyt->xyctz/dot_general | solution.py:111
  183.1 10.5 %copy.34 = bf16[32,32,32,2,16]{2,4,3,1,0:T(8,128)(2,1)} copy(bf16[32,32,32,2,16]{2,1,4,0,3:T(8,128)(2,1)} %fusion.12) | data formatting | bytes 4194304 | tf_op jit(solution)/shard_map/convert_element_type | solution.py:113
  193.6 14.5 %fusion.93 = (f32[32,32,128]{2,1,0:T(8,128)S(1)}, f32[32,32,32,128]{3,2,1,0:T(8,128)}) fusion(f32[32]{0:T(128)S(1)} %bitcast.164, f32[32,32,128,32]{2,3,1,0:T(8,128)} %fusion.13, bf16[32,32,32,32]{2,3,1,0:T(8,128)(2,1)} %bitcast.160, bf16[16,128]{1,0:T(8,128)(2,1)S(1)} %get-tuple-element.41, bf16[16,128]{1,0:T(8,128)(2,1)S(1)} %get-tuple-element.42), kind=kOutput, calls=%fused_computation.167 | convolution fusion | flops 285097984 | bytes 36184192 | tf_op jit(solution)/shard_map/dot_general | solution.py:114
  208.2 10.9 %multiply_reduce_fusion = f32[32,32,128]{2,1,0:T(8,128)S(1)} fusion(f32[32,32,32,128]{3,2,1,0:T(8,128)} %get-tuple-element.36, f32[32,32,128]{2,1,0:T(8,128)S(1)} %broadcast_multiply_fusion), kind=kLoop, calls=%fused_computation.23 | loop fusion | flops 12451840 | bytes 17825792 | tf_op jit(solution)/shard_map/reduce_sum | solution.py:69
  219.1 0.1 add_rsqrt_fusion
  219.2 41.4 %fusion.21 = bf16[1,32,32,32,128]{4,3,2,1,0:T(8,128)(2,1)} fusion(f32[32]{0:T(128)S(1)} %bitcast.162, f32[32]{0:T(128)S(1)} %bitcast.163, f32[32,32,128]{2,1,0:T(8,128)S(1)} %add_rsqrt_fusion, f32[32,32,32,128]{3,2,1,0:T(8,128)} %get-tuple-element.36, f32[32,32,128]{2,1,0:T(8,128)S(1)} %broadcast_multiply_fusion), kind=kLoop, calls=%fused_computation.36 | loop fusion | flops 289406976 | bytes 26214656 | tf_op jit(solution)/shard_map/broadcast_in_dim | solution.py:124
  (26 shorter events, 0.3 us)
Async XLA Ops:
  7.4 23.4 %copy-start = (bf16[1,32,32]{2,1,0:T(8,128)(2,1)S(1)}, bf16[1,32,32]{2,1,0:T(8,128)(2,1)}, u32[]{:S(2)}) copy-start(bf16[1,32,32]{2,1,0:T(8,128)(2,1)} %param.8) | copy-start | bytes 6148
  7.4 69.8 %reduce-scatter.3.cloned.1.call-start = ((), (), s32[]{:S(2)}) async-start(), calls=%async_computation.2 | async-start | bytes 5242880 | tf_op jit(solution)/shard_map/reduce_scatter | solution.py:95
  29.7 61.4 %all-gather.3.cloned.1.call-start = ((), (), s32[]{:S(2)}) async-start(), calls=%async_computation.4 | async-start | bytes 6291456 | tf_op jit(solution)/shard_map/all_gather | solution.py:103
  30.3 72.8 %reduce-scatter.5.cloned.1.call-start = ((), (), s32[]{:S(2)}) async-start(), calls=%async_computation.3 | async-start | bytes 655360 | tf_op jit(solution)/shard_map/reduce_scatter | solution.py:99
  160.3 33.3 %copy-start.4 = (f32[1,32]{1,0:T(1,128)S(1)}, f32[1,32]{1,0:T(1,128)}, u32[]{:S(2)}) copy-start(f32[1,32]{1,0:T(1,128)} %param.9) | copy-start | bytes 388
  208.1 11.1 %copy-start.2 = (f32[1,32]{1,0:T(1,128)S(1)}, f32[1,32]{1,0:T(1,128)}, u32[]{:S(2)}) copy-start(f32[1,32]{1,0:T(1,128)} %param.11) | copy-start | bytes 388
  208.1 11.1 %copy-start.3 = (f32[1,32]{1,0:T(1,128)S(1)}, f32[1,32]{1,0:T(1,128)}, u32[]{:S(2)}) copy-start(f32[1,32]{1,0:T(1,128)} %param.10) | copy-start | bytes 388
  208.2 52.5 %copy-start.1 = (bf16[1,32,32]{2,1,0:T(8,128)(2,1)S(1)}, bf16[1,32,32]{2,1,0:T(8,128)(2,1)}, u32[]{:S(2)}) copy-start(bf16[1,32,32]{2,1,0:T(8,128)(2,1)} %param.8) | copy-start | bytes 6148
Sparse Core Ops, SparseCore 0:
  29.9 47.2 reduce-scatter.2
  80.2 21.8 reduce-scatter.4
Sparse Core Ops, SparseCore 1:
  31.8 59.3 all-gather.2
where the time goes:
time: 269 us; the launch traced here: 268 us
  matrix products  75.9 us (28%)
  other arithmetic  53 us (20%)
  blocking collectives  45.7 us (17%)
  waiting for transfers between devices  42.8 us (16%)
  local copies, waits for them, and re-layouts  35.4 us (13%)
  between operations  15 us (6%)
    broadcast_in_dim x1, other arithmetic, local(): return hidden[None]  41.4 us
    all_gather x1, blocking collectives, local(): full_modes = lax.all_gather(gathered_second, 'gx', axis=0, tiled=True)  38.6 us
    reduce_scatter x1, waiting for transfers between devices, local(): lax.psum_scatter(along_second.astype(jnp.bfloat16), 'gy', scatter_dimensi...  31.2 us
    dot_general x1, matrix products, local(): jnp.einsum('xkcsz,ksyt->xyctz', rows_first, second_inverse, precision=hig...  22.8 us
    dot_general x1, matrix products, local(): jnp.einsum('oc,xycz->xyoz', skip_weight[0], hidden, preferred_element_typ...  15.1 us
    dot_general x1, matrix products, local(): jnp.dot(rows_both.reshape(-1, 2 * MZ), depth_backward, preferred_element_...  14.5 us
    all_gather x1, waiting for transfers between devices, local(): lax.all_gather(weights_here, 'col', axis=4, tiled=True)  11 us
    reduce_sum x1, other arithmetic, finish(): spread = jnp.mean(jnp.square(pre_norm - centre), axis=2, keepdims=True)  10.9 us
  transfers between devices with their start and end apart: 3, of which 2 were waited for; matrix products, arithmetic and copies ran while one was open for 11% of the time, Pallas kernels for 0%

commit v1 on v0

--- a/solution.py
+++ b/solution.py
@@ -104,10 +104,37 @@
         jnp.bfloat16
     )
     gathered_second = lax.all_gather(mixed_modes, "gy", axis=1, tiled=True)
-    full_modes = lax.all_gather(gathered_second, "gx", axis=0, tiled=True)
+    length_2, place, rows = (lax.axis_size("gx"), lax.axis_index("gx"), gathered_second.shape[0])
+    route = [(i, (i + 1) % length_2) for i in range(length_2)]
+    behind = [(i, (i - 1) % length_2) for i in range(length_2)]
+    half = length_2 // 2
+    from_left = from_right = gathered_second
     rows_first = jnp.einsum(
-        "jkcsz,jsxt->xkctz", full_modes, first_inverse, preferred_element_type=jnp.float32
+        "jkcsz,jsxt->xkctz",
+        gathered_second,
+        lax.dynamic_slice_in_dim(first_inverse, place * rows, gathered_second.shape[0], axis=0),
+        preferred_element_type=jnp.float32,
     )
+    for step in range(1, half + 1):
+        from_left = lax.ppermute(from_left, "gx", route)
+        if step < length_2 - half:
+            from_right = lax.ppermute(from_right, "gx", behind)
+            rows_first = rows_first + jnp.einsum(
+                "jkcsz,jsxt->xkctz",
+                from_right,
+                lax.dynamic_slice_in_dim(
+                    first_inverse, (place + step) % length_2 * rows, from_right.shape[0], axis=0
+                ),
+                preferred_element_type=jnp.float32,
+            )
+        rows_first = rows_first + jnp.einsum(
+            "jkcsz,jsxt->xkctz",
+            from_left,
+            lax.dynamic_slice_in_dim(
+                first_inverse, (place - step) % length_2 * rows, from_left.shape[0], axis=0
+            ),
+            preferred_element_type=jnp.float32,
+        )
     rows_both = jnp.einsum(
         "xkcsz,ksyt->xyctz", rows_first, second_inverse, precision=highest
     ).astype(jnp.bfloat16)

time: 269 us -> 284 us (1.056); the launches traced: 268 us -> 279 us
  blocking collectives: 45.7 us -> 7.15 us
  waiting for transfers between devices: 42.8 us -> 68.8 us
  matrix products: 75.9 us -> 93.1 us
  starting transfers between devices: 0.27 us -> 5.59 us
    all_gather x1 -> x0, blocking collectives: 38.6 us -> none  [local(): full_modes = lax.all_gather(gathered_second, 'gx', axis=0, tiled=True)]
    ppermute x0 -> x3, waiting for transfers between devices: none -> 26.4 us  [the longest x2 26.4 us: local(): from_left = lax.ppermute(from_left, 'gx', route)]
    dot_general x1 -> x4, matrix products: 1.49 us -> 18.6 us  [the longest x2 12.4 us: local(): jnp.einsum('jkcsz,jsxt->xkctz', from_left, lax.dynamic_slice_in_dim(first...]
    ppermute x0 -> x3, starting transfers between devices: none -> 5.04 us  [the longest x1 3.37 us: local(): from_right = lax.ppermute(from_right, 'gx', behind)]
  transfers between devices with their start and end apart: 3 -> 6, of which waited for: 2 -> 4; matrix products, arithmetic and copies ran while one was open for 11% -> 15% of each run, Pallas kernels for 0% -> 0%
where the time goes in v1:
time: 284 us; the launch traced here: 279 us
  matrix products  93.1 us (33%)
  waiting for transfers between devices  68.8 us (24%)
  other arithmetic  53 us (19%)
  local copies, waits for them, and re-layouts  35.7 us (13%)
  between operations  15.4 us (5%)
  blocking collectives  7.15 us (3%)
  starting transfers between devices  5.59 us (2%)
    broadcast_in_dim x1, other arithmetic, local(): return hidden[None]  41.4 us
    reduce_scatter x1, waiting for transfers between devices, local(): lax.psum_scatter(along_second.astype(jnp.bfloat16), 'gy', scatter_dimensi...  30.7 us
    ppermute x2, waiting for transfers between devices, local(): from_left = lax.ppermute(from_left, 'gx', route)  26.4 us
    dot_general x1, matrix products, local(): jnp.einsum('xkcsz,ksyt->xyctz', rows_first, second_inverse, precision=hig...  22.8 us
    dot_general x1, matrix products, local(): jnp.einsum('oc,xycz->xyoz', skip_weight[0], hidden, preferred_element_typ...  15.2 us
    dot_general x1, matrix products, local(): jnp.dot(rows_both.reshape(-1, 2 * MZ), depth_backward, preferred_element_...  14.4 us
    dot_general x2, matrix products, local(): jnp.einsum('jkcsz,jsxt->xkctz', from_left, lax.dynamic_slice_in_dim(first...  12.4 us
    all_gather x1, waiting for transfers between devices, local(): lax.all_gather(weights_here, 'col', axis=4, tiled=True)  11 us
  transfers between devices with their start and end apart: 6, of which 4 were waited for; matrix products, arithmetic and copies ran while one was open for 15% of the time, Pallas kernels for 0%

profile of v1, /device:TPU:0, one launch (start us, length us, event | category | flops | bytes accessed | tf_op | source)
XLA Modules:
  0.0 278.6 jit_solution(12082684635463805351)
XLA Ops:
  7.4 6.4 %fusion = bf16[32768,32]{0,1:T(8,128)(2,1)S(1)} fusion(bf16[32768,128]{1,0:T(8,128)(2,1)} %bitcast.198, bf16[128,16]{0,1:T(8,128)(2,1)S(1)} %get-tuple-element.37, bf16[128,16]{0,1:T(8,128)(2,1)S(1)} %get-tuple-element.38), kind=kOutput, calls=%fused_computation.1 | convolution fusion | flops 269500416 | bytes 10493952 | tf_op jit(solution)/shard_map/dot_general | solution.py:88
  13.8 7.9 %reshape.722 = bf16[32,32,32,2,16]{2,1,0,4,3:T(8,128)(2,1)} reshape(bf16[32768,32]{0,1:T(8,128)(2,1)S(1)} %fusion) | data formatting | bytes 4194304 | tf_op jit(solution)/shard_map/reshape | solution.py:91
  21.9 4.7 %fusion.25 = bf16[32,16,32,2,16]{2,1,4,0,3:T(8,128)(2,1)S(1)} fusion(bf16[32,32,32,2,16]{2,1,0,4,3:T(8,128)(2,1)} %reshape.722, bf16[32,1,16,2]{0,2,1,3:T(8,128)(2,1)S(1)} %get-tuple-element.16, bf16[32,1,16,2]{0,2,1,3:T(8,128)(2,1)S(1)} %get-tuple-element.15), kind=kOutput, calls=%fused_computation.41 | convolution fusion | flops 67641344 | bytes 3149824 | tf_op jit(solution)/shard_map/xycrz,yrks->xkcsz/dot_general | solution.py:92
  26.6 3.1 %copy.26 = bf16[32,16,32,2,16]{2,4,3,0,1:T(8,128)(2,1)} copy(bf16[32,16,32,2,16]{2,1,4,0,3:T(8,128)(2,1)S(1)} %fusion.25) | data formatting | bytes 2097152 | tf_op jit(solution)/shard_map/convert_element_type | solution.py:96
  29.8 0.5 all-gather.3.cloned.1.call-update
  31.2 15.2 %fusion.13 = f32[32,32,128,32]{2,3,1,0:T(8,128)} fusion(bf16[1,32,32,32,128]{4,3,2,1,0:T(8,128)(2,1)} %param.6, bf16[1,32,32]{2,1,0:T(8,128)(2,1)S(1)} %copy-done), kind=kOutput, calls=%fused_computation.27 | convolution fusion | flops 268435456 | bytes 25167872 | tf_op jit(solution)/shard_map/oc,xycz->xyoz/dot_general | solution.py:147
  46.4 30.7 %reduce-scatter.3.cloned.1.call-done = bf16[32,4,32,2,16]{2,4,3,0,1:T(8,128)(2,1)} async-done(((bf16[32,16,32,2,16]{2,4,3,0,1:T(8,128)(2,1)}), bf16[32,4,32,2,16]{2,4,3,0,1:T(8,128)(2,1)}) %reduce-scatter.3.cloned.1.call-update) | async-done | bytes 262160 | tf_op jit(solution)/shard_map/reduce_scatter | solution.py:95
  77.2 1.9 fusion.29
  79.1 0.9 copy.29
  80.1 11.0 %all-gather.3.cloned.1.call-done = bf16[1,4,4,2,32,32,16]{4,6,5,3,2,1,0:T(8,128)(2,1)} async-done(((bf16[1,4,4,2,32,16,16]{4,6,5,3,2,1,0:T(8,128)(2,1)}), bf16[1,4,4,2,32,32,16]{4,6,5,3,2,1,0:T(8,128)(2,1)}) %all-gather.3.cloned.1.call-update) | async-done | bytes 1048592 | tf_op jit(solution)/shard_map/all_gather | solution.py:103
  91.1 4.5 %slice_bitcast_fusion = (bf16[4,4,32,32,16]{2,4,3,1,0:T(8,128)(2,1)}, bf16[4,4,32,32,16]{2,4,3,1,0:T(8,128)(2,1)S(1)}) fusion(bf16[4,4,2,32,32,16]{3,5,4,2,1,0:T(8,128)(2,1)} %bitcast.200), kind=kLoop, calls=%fused_computation.42 | loop fusion | bytes 2097152 | tf_op jit(solution)/shard_map/squeeze | solution.py:60
  95.6 4.5 %copy.45 = bf16[4,4,32,32,16]{3,2,4,1,0:T(8,128)(2,1)} copy(bf16[4,4,32,32,16]{2,4,3,1,0:T(8,128)(2,1)} %get-tuple-element.5) | data formatting | bytes 1048576 | tf_op jit(solution)/shard_map/squeeze | solution.py:60
  100.2 2.9 %copy.42 = bf16[4,4,32,32,16]{3,2,4,1,0:T(8,128)(2,1)} copy(bf16[4,4,32,32,16]{2,4,3,1,0:T(8,128)(2,1)S(1)} %get-tuple-element.6) | data formatting | bytes 1048576 | tf_op jit(solution)/shard_map/squeeze | solution.py:59
  103.1 0.9 slice_bitcast_fusion.3
  104.0 2.2 fusion.43
  106.2 2.2 fusion.41
  108.5 2.3 fusion.47
  110.7 2.3 fusion.45
  113.1 7.2 %all_gather.7 = bf16[4,16,32,2,16]{2,4,3,0,1:T(8,128)(2,1)S(1)} all-gather(bf16[4,4,32,2,16]{2,4,3,0,1:T(8,128)(2,1)S(1)} %pad_maximum_fusion), channel_id=1, replica_groups=mesh['gx'=4,'gy'=4,'col'=2] {'gy'}, dimensions={1}, use_global_device_ids=true | all-gather | bytes 163840 | tf_op jit(solution)/shard_map/all_gather | solution.py:106
  120.5 3.4 %collective-permute-start = (bf16[4,16,32,2,16]{2,0,3,4,1:T(4,128)(2,1)S(1)}, bf16[4,16,32,2,16]{2,0,3,4,1:T(4,128)(2,1)S(1)}, u32[]{:S(2)}, u32[]{:S(2)}) collective-permute-start(bf16[4,16,32,2,16]{2,0,3,4,1:T(4,128)(2,1)S(1)} %copy.30), channel_id=1, source_target_pairs={{0,24},{8,0},{16,8},{24,16},{1,25},{9,1},{17,9},{25,17},{2,26},{10... | collective-permute-start | bytes 393224 | tf_op jit(solution)/shard_map/ppermute | solution.py:121
  123.9 1.5 fusion.37
  125.4 22.5 %collective-permute-done.1 = bf16[4,16,32,2,16]{2,0,3,4,1:T(4,128)(2,1)S(1)} collective-permute-done((bf16[4,16,32,2,16]{2,0,3,4,1:T(4,128)(2,1)S(1)}, bf16[4,16,32,2,16]{2,0,3,4,1:T(4,128)(2,1)S(1)}, u32[]{:S(2)}, u32[]{:S(2)}) %collective-permute-start.1) | collective-permute-done | bytes 131104 | tf_op jit(solution)/shard_map/ppermute | solution.py:119
  147.8 1.7 collective-permute-start.2
  149.5 4.9 %fusion.33 = f32[32,2,16,32,16,1]{3,0,5,4,2,1:T(8,128)} fusion(bf16[4,16,32,2,16]{2,0,3,4,1:T(4,128)(2,1)S(1)} %collective-permute-done.1, s32[]{:T(128)S(6)} %select_n.148, bf16[16,1,32,2]{2,0,1,3:T(8,128)(2,1)S(1)} %get-tuple-element.14, bf16[16,1,32,2]{2,0,1,3:T(8,128)(2,1)S(1)} %get-tuple-element.13), kind=kOutput, calls=%fused_computation.50 | convolution fusion | flops 8390656 | bytes 2232324 | tf_op jit(solution)/shard_map/jkcsz,jsxt->xkctz/dot_general | solution.py:130
  154.4 4.7 %fusion.35 = f32[32,2,16,32,16,1]{3,0,5,4,2,1:T(8,128)} fusion(bf16[4,16,32,2,16]{2,0,3,4,1:T(4,128)(2,1)S(1)} %collective-permute-done, s32[]{:T(128)S(6)} %select_n.146, bf16[16,1,32,2]{2,0,1,3:T(8,128)(2,1)S(1)} %get-tuple-element.14, bf16[16,1,32,2]{2,0,1,3:T(8,128)(2,1)S(1)} %get-tuple-element.13), kind=kOutput, calls=%fused_computation.52 | convolution fusion | flops 8390656 | bytes 2232324 | tf_op jit(solution)/shard_map/jkcsz,jsxt->xkctz/dot_general | solution.py:122
  159.1 4.0 %collective-permute-done.2 = bf16[4,16,32,2,16]{2,0,3,4,1:T(4,128)(2,1)S(1)} collective-permute-done((bf16[4,16,32,2,16]{2,0,3,4,1:T(4,128)(2,1)S(1)}, bf16[4,16,32,2,16]{2,0,3,4,1:T(4,128)(2,1)S(1)}, u32[]{:S(2)}, u32[]{:S(2)}) %collective-permute-start.2) | collective-permute-done | bytes 131104 | tf_op jit(solution)/shard_map/ppermute | solution.py:119
  163.1 7.6 %fusion.17 = f32[32,16,32,2,16]{2,0,4,1,3:T(8,128)S(1)} fusion(f32[32,2,16,32,16,1]{3,0,5,4,2,1:T(8,128)} %fusion.33, f32[32,2,16,32,16,1]{3,0,5,4,2,1:T(8,128)} %fusion.35, f32[32,2,16,32,16,1]{3,0,5,4,2,1:T(8,128)S(1)} %fusion.37, bf16[4,16,32,2,16]{2,0,3,4,1:T(4,128)(2,1)S(1)} %collective-permute-done.2, s32[]{:T(128)S(6)} %select_n.150, ...), kind=kOutput, calls=%fused_computation.32 | convolution fusion | flops 9963520 | bytes 8523780 | tf_op jit(solution)/shard_map/jkcsz,jsxt->xkctz/dot_general | solution.py:130
  170.7 22.8 %fusion.12 = bf16[32,32,32,2,16]{2,1,4,0,3:T(8,128)(2,1)} fusion(f32[32,16,32,2,16]{2,0,4,1,3:T(8,128)S(1)} %fusion.17, f32[16,1,32,2]{2,0,3,1:T(8,128)S(1)} %get-tuple-element.10, f32[16,1,32,2]{2,0,3,1:T(8,128)S(1)} %get-tuple-element.9), kind=kOutput, calls=%fused_computation.26 | convolution fusion | flops 403703808 | bytes 4202496 | tf_op jit(solution)/shard_map/xkcsz,ksyt->xyctz/dot_general | solution.py:138
  193.4 10.5 %copy.35 = bf16[32,32,32,2,16]{2,4,3,1,0:T(8,128)(2,1)} copy(bf16[32,32,32,2,16]{2,1,4,0,3:T(8,128)(2,1)} %fusion.12) | data formatting | bytes 4194304 | tf_op jit(solution)/shard_map/convert_element_type | solution.py:140
  204.0 14.4 %fusion.117 = (f32[32,32,128]{2,1,0:T(8,128)S(1)}, f32[32,32,32,128]{3,2,1,0:T(8,128)}) fusion(f32[32]{0:T(128)S(1)} %bitcast.203, f32[32,32,128,32]{2,3,1,0:T(8,128)} %fusion.13, bf16[32,32,32,32]{2,3,1,0:T(8,128)(2,1)} %bitcast.199, bf16[16,128]{1,0:T(8,128)(2,1)S(1)} %get-tuple-element.41, bf16[16,128]{1,0:T(8,128)(2,1)S(1)} %get-tuple-element.42), kind=kOutput, calls=%fused_computation.196 | convolution fusion | flops 285097984 | bytes 36184192 | tf_op jit(solution)/shard_map/dot_general | solution.py:141
  218.5 10.9 %multiply_reduce_fusion = f32[32,32,128]{2,1,0:T(8,128)S(1)} fusion(f32[32,32,32,128]{3,2,1,0:T(8,128)} %get-tuple-element.36, f32[32,32,128]{2,1,0:T(8,128)S(1)} %broadcast_multiply_fusion), kind=kLoop, calls=%fused_computation.23 | loop fusion | flops 12451840 | bytes 17825792 | tf_op jit(solution)/shard_map/reduce_sum | solution.py:69
  229.5 41.4 %fusion.22 = bf16[1,32,32,32,128]{4,3,2,1,0:T(8,128)(2,1)} fusion(f32[32]{0:T(128)S(1)} %bitcast.201, f32[32]{0:T(128)S(1)} %bitcast.202, f32[32,32,128]{2,1,0:T(8,128)S(1)} %add_rsqrt_fusion, f32[32,32,32,128]{3,2,1,0:T(8,128)} %get-tuple-element.36, f32[32,32,128]{2,1,0:T(8,128)S(1)} %broadcast_multiply_fusion), kind=kLoop, calls=%fused_computation.40 | loop fusion | flops 289406976 | bytes 26214656 | tf_op jit(solution)/shard_map/broadcast_in_dim | solution.py:151
  (34 shorter events, 1.6 us)
Async XLA Ops:
  7.4 23.8 %copy-start = (bf16[1,32,32]{2,1,0:T(8,128)(2,1)S(1)}, bf16[1,32,32]{2,1,0:T(8,128)(2,1)}, u32[]{:S(2)}) copy-start(bf16[1,32,32]{2,1,0:T(8,128)(2,1)} %param.8) | copy-start | bytes 6148
  7.4 69.8 %reduce-scatter.3.cloned.1.call-start = ((), (), s32[]{:S(2)}) async-start(), calls=%async_computation.2 | async-start | bytes 5242880 | tf_op jit(solution)/shard_map/reduce_scatter | solution.py:95
  29.7 61.4 %all-gather.3.cloned.1.call-start = ((), (), s32[]{:S(2)}) async-start(), calls=%async_computation.4 | async-start | bytes 6291456 | tf_op jit(solution)/shard_map/all_gather | solution.py:103
  30.3 72.8 %reduce-scatter.5.cloned.1.call-start = ((), (), s32[]{:S(2)}) async-start(), calls=%async_computation.3 | async-start | bytes 655360 | tf_op jit(solution)/shard_map/reduce_scatter | solution.py:99
  120.5 33.9 %collective-permute-start = (bf16[4,16,32,2,16]{2,0,3,4,1:T(4,128)(2,1)S(1)}, bf16[4,16,32,2,16]{2,0,3,4,1:T(4,128)(2,1)S(1)}, u32[]{:S(2)}, u32[]{:S(2)}) collective-permute-start(bf16[4,16,32,2,16]{2,0,3,4,1:T(4,128)(2,1)S(1)} %copy.30), channel_id=1, source_target_pairs={{0,24},{8,0},{16,8},{24,16},{1,25},{9,1},{17,9},{25,17},{2,26},{10... | collective-permute-start | bytes 393224 | tf_op jit(solution)/shard_map/ppermute | solution.py:121
  123.9 23.9 %collective-permute-start.1 = (bf16[4,16,32,2,16]{2,0,3,4,1:T(4,128)(2,1)S(1)}, bf16[4,16,32,2,16]{2,0,3,4,1:T(4,128)(2,1)S(1)}, u32[]{:S(2)}, u32[]{:S(2)}) collective-permute-start(bf16[4,16,32,2,16]{2,0,3,4,1:T(4,128)(2,1)S(1)} %copy.30), channel_id=1, source_target_pairs={{0,8},{8,16},{16,24},{24,0},{1,9},{9,17},{17,25},{25,1},{2,10},{10... | collective-permute-start | bytes 393224 | tf_op jit(solution)/shard_map/ppermute | solution.py:119
  147.8 15.3 %collective-permute-start.2 = (bf16[4,16,32,2,16]{2,0,3,4,1:T(4,128)(2,1)S(1)}, bf16[4,16,32,2,16]{2,0,3,4,1:T(4,128)(2,1)S(1)}, u32[]{:S(2)}, u32[]{:S(2)}) collective-permute-start(bf16[4,16,32,2,16]{2,0,3,4,1:T(4,128)(2,1)S(1)} %collective-permute-done.1), channel_id=1, source_target_pairs={{0,8},{8,16},{16,24},{24,0},{1,9},{9,17},{17,25},{25,1},{2,10},{10... | collective-permute-start | bytes 393224 | tf_op jit(solution)/shard_map/ppermute | solution.py:119
  170.7 33.3 %copy-start.4 = (f32[1,32]{1,0:T(1,128)S(1)}, f32[1,32]{1,0:T(1,128)}, u32[]{:S(2)}) copy-start(f32[1,32]{1,0:T(1,128)} %param.9) | copy-start | bytes 388
  218.4 11.1 %copy-start.2 = (f32[1,32]{1,0:T(1,128)S(1)}, f32[1,32]{1,0:T(1,128)}, u32[]{:S(2)}) copy-start(f32[1,32]{1,0:T(1,128)} %param.11) | copy-start | bytes 388
  218.4 11.1 %copy-start.3 = (f32[1,32]{1,0:T(1,128)S(1)}, f32[1,32]{1,0:T(1,128)}, u32[]{:S(2)}) copy-start(f32[1,32]{1,0:T(1,128)} %param.10) | copy-start | bytes 388
  218.5 52.5 %copy-start.1 = (bf16[1,32,32]{2,1,0:T(8,128)(2,1)S(1)}, bf16[1,32,32]{2,1,0:T(8,128)(2,1)}, u32[]{:S(2)}) copy-start(bf16[1,32,32]{2,1,0:T(8,128)(2,1)} %param.8) | copy-start | bytes 6148
Sparse Core Ops, SparseCore 0:
  29.9 47.2 reduce-scatter.2
  80.2 21.8 reduce-scatter.4
Sparse Core Ops, SparseCore 1:
  31.8 59.3 all-gather.2
